TPU v7x, 32 devices: a whole 2x2x4 slice. The times are simulated.
32 devices in a mesh: gx: 4 (over y, core), gy: 2 (over x), gz: 4 (over z).
Axes of the slice: x: 2, y: 2, z: 4, core: 2. Of those that a mesh axis runs over, the one named last changes fastest.
Arguments:
- old_basis: float32 [4, 32, 32, 512], P(None, 'gx', 'gy', 'gz'), may hold values from -4 to 4, as said below
- previous: float32 [4, 32, 32, 512], P(None, 'gx', 'gy', 'gz'), as said below
- incoming: float32 [4, 32, 32, 512], P(None, 'gx', 'gy', 'gz'), may hold values from -6 to 6
- coefficient: float32 [32, 32, 512], P('gx', 'gy', 'gz'), may hold values from 0.5 to 4
Outputs:
- orthonormal: float32 [4, 32, 32, 512], P(None, 'gx', 'gy', 'gz')
- projection: float32 [4, 4], replicated
- triangle: float32 [4, 4], replicated
- preconditioned: float32 [4, 32, 32, 512], P(None, 'gx', 'gy', 'gz')
- operated: float32 [4, 32, 32, 512], P(None, 'gx', 'gy', 'gz')
Inputs may be any that keep to these rules, and one draw needn't show every extreme that they name: `old_basis`: entries of order one; the basis vectors are independent, so every Gram matrix formed from them is well conditioned. `previous`: entries of order one; each vector has a part outside the span of old_basis of norm of order one under the inner product.
All inputs are finite; a program needn't handle non-finite values.
Results may differ from a plain program's by a relative error of at most 0.0003.
Values sent between devices are 32-bit elements; how exact they have to be, the bound alone decides.
No kernel may reach another device: no remote copies, remote signals or barrier semaphores. Data moves between devices by JAX's collectives and lax.ppermute only.
A program may use at most 64 MiB of HBM per device.

v0:
```python
import jax
import jax.numpy as jnp
from jax import lax
from jax.sharding import PartitionSpec as P

LEVELS = 6
COARSE_SWEEPS = 4
OMEGA = 0.8
HIGH = lax.Precision.HIGHEST


def with_halo(shard, sides, width):
    for axis, dim in sides:
        count, length = (lax.axis_size(axis), shard.shape[dim])
        up = [(i, (i + 1) % count) for i in range(count - 1)]
        down = [(j, i) for i, j in up]
        last = lax.slice_in_dim(shard, length - width, length, axis=dim)
        leading = lax.slice_in_dim(shard, 0, width, axis=dim)
        before = lax.ppermute(last, axis, up)
        after = lax.ppermute(leading, axis, down)
        shard = jnp.concatenate([before, shard, after], axis=dim)
    return shard


def stencil(extended, coeffs, factor):
    center = extended[:, 1:-1, 1:-1, 1:-1]
    total = extended[:, 2:, 1:-1, 1:-1] + extended[:, :-2, 1:-1, 1:-1]
    total = total + extended[:, 1:-1, 2:, 1:-1] + extended[:, 1:-1, :-2, 1:-1]
    total = total + extended[:, 1:-1, 1:-1, 2:] + extended[:, 1:-1, 1:-1, :-2]
    return factor * coeffs * (6.0 * center - total)


def zero_margin(field):
    return jnp.pad(field, ((0, 0), (1, 1), (1, 1), (1, 1)))


def with_faces(field):
    return with_halo(field, (("gx", 1), ("gy", 2), ("gz", 3)), 1)


def restrict(field):
    depth, size_a, size_b, size_c = field.shape
    return field.reshape(depth, size_a // 2, 2, size_b // 2, 2, size_c // 2, 2).mean(axis=(2, 4, 6))


def prolong(field):
    return jnp.repeat(jnp.repeat(jnp.repeat(field, 2, axis=1), 2, axis=2), 2, axis=3)


def whole_cycle(source, coeff_list, level):
    coeffs = coeff_list[level]
    factor = 0.25**level
    diagonal = 6.0 * factor * coeffs
    iterate = OMEGA * source / diagonal
    if level == LEVELS - 1:
        for sweep in range(COARSE_SWEEPS - 1):
            iterate = (
                iterate
                + OMEGA * (source - stencil(zero_margin(iterate), coeffs, factor)) / diagonal
            )
        return iterate
    iterate = iterate + OMEGA * (source - stencil(zero_margin(iterate), coeffs, factor)) / diagonal
    residue = source - stencil(zero_margin(iterate), coeffs, factor)
    iterate = iterate + prolong(whole_cycle(restrict(residue), coeff_list, level + 1))
    iterate = iterate + OMEGA * (source - stencil(zero_margin(iterate), coeffs, factor)) / diagonal
    return iterate


def agglomerate(source, coeffs, start_level):
    vectors = source.shape[0]
    stacked = jnp.concatenate([source, coeffs[None]], axis=0)
    depth, size_a, size_b, size_c = stacked.shape
    flattened = stacked.reshape(depth, size_a * size_b * size_c)
    gathered = lax.all_gather(flattened, ("gx", "gy", "gz"), axis=1, tiled=True)
    count_x, count_y, count_z = (lax.axis_size("gx"), lax.axis_size("gy"), lax.axis_size("gz"))
    gathered = gathered.reshape(depth, count_x, count_y, count_z, size_a, size_b, size_c)
    gathered = gathered.transpose(0, 1, 4, 2, 5, 3, 6).reshape(
        depth, count_x * size_a, count_y * size_b, count_z * size_c
    )
    coarse_list = [gathered[vectors]]
    for level in range(LEVELS - 1 - start_level):
        coarse_list.append(restrict(coarse_list[-1][None])[0])
    solution = whole_cycle(gathered[:vectors], [None] * start_level + coarse_list, start_level)
    starts = (
        jnp.zeros((), jnp.int32),
        lax.axis_index("gx") * size_a,
        lax.axis_index("gy") * size_b,
        lax.axis_index("gz") * size_c,
    )
    return lax.dynamic_slice(solution, starts, (vectors, size_a, size_b, size_c))


def local_cycle(source, coeff_list, level, start_level):
    coeffs = coeff_list[level]
    if level == start_level:
        return agglomerate(source, coeffs, start_level)
    factor = 0.25**level
    diagonal = 6.0 * factor * coeffs
    vectors = source.shape[0]
    stacked = jnp.concatenate([source, coeffs[None]], axis=0)
    widened = with_halo(stacked, (("gx", 1), ("gy", 2), ("gz", 3)), 2)
    source_wide = widened[:vectors]
    coeff_wide = widened[vectors]
    safe_wide = jnp.where(coeff_wide > 0.0, coeff_wide, 1.0)
    sweep_one = OMEGA * source_wide / (6.0 * factor * safe_wide)
    inner_coeff = coeff_wide[1:-1, 1:-1, 1:-1]
    inner_safe = safe_wide[1:-1, 1:-1, 1:-1]
    sweep_two = sweep_one[:, 1:-1, 1:-1, 1:-1] + OMEGA * (
        source_wide[:, 1:-1, 1:-1, 1:-1] - stencil(sweep_one, inner_coeff, factor)
    ) / (6.0 * factor * inner_safe)
    iterate = sweep_two[:, 1:-1, 1:-1, 1:-1]
    residue = source - stencil(sweep_two, coeffs, factor)
    iterate = iterate + prolong(local_cycle(restrict(residue), coeff_list, level + 1, start_level))
    iterate = iterate + OMEGA * (source - stencil(with_faces(iterate), coeffs, factor)) / diagonal
    return iterate


def triangular_inverse(lower):
    order = lower.shape[0]
    identity = jnp.eye(order, dtype=lower.dtype)
    inverse = jnp.zeros_like(lower)
    for row in range(order):
        values = identity[row] - jnp.dot(lower[row, :row], inverse[:row], precision=HIGH)
        inverse = inverse.at[row].set(values / lower[row, row])
    return inverse


def per_device(old_basis, previous, incoming, coefficient):
    local_cells = old_basis.shape[1] * old_basis.shape[2] * old_basis.shape[3]
    total_cells = float(
        local_cells * lax.axis_size("gx") * lax.axis_size("gy") * lax.axis_size("gz")
    )
    basis_local = jnp.einsum("mxyz,jxyz->mj", old_basis, previous, precision=HIGH)
    projection = lax.psum(basis_local, ("gx", "gy", "gz")) / total_cells
    remainder = previous - jnp.einsum("mxyz,mj->jxyz", old_basis, projection, precision=HIGH)
    gram_local = jnp.einsum("ixyz,jxyz->ij", remainder, remainder, precision=HIGH)
    gram = lax.psum(gram_local, ("gx", "gy", "gz")) / total_cells
    start_level = LEVELS - 3
    coeff_list = [coefficient]
    for level in range(start_level):
        coeff_list.append(restrict(coeff_list[-1][None])[0])
    preconditioned = local_cycle(incoming, coeff_list, 0, start_level)
    operated = stencil(with_faces(preconditioned), coefficient, 1.0)
    lower = jnp.linalg.cholesky(gram)
    inverse = triangular_inverse(lower)
    orthonormal = jnp.einsum("ji,ixyz->jxyz", inverse, remainder, precision=HIGH)
    return (orthonormal, projection, lower.T, preconditioned, operated)


def solution(mesh):
    in_specs = (
        P(None, "gx", "gy", "gz"),
        P(None, "gx", "gy", "gz"),
        P(None, "gx", "gy", "gz"),
        P("gx", "gy", "gz"),
    )
    out_specs = (
        P(None, "gx", "gy", "gz"),
        P(),
        P(),
        P(None, "gx", "gy", "gz"),
        P(None, "gx", "gy", "gz"),
    )
    return jax.shard_map(
        per_device, mesh=mesh, in_specs=in_specs, out_specs=out_specs, check_vma=False
    )
```

profile of v0, /device:TPU:25, one launch (start us, length us, event | category | flops | bytes accessed | tf_op | source)
XLA Modules:
  0.0 369.9 jit_solution(2257460580880497571)
XLA Ops:
  1.6 3.7 %collective-permute-start = (f32[5,2,16,128]{3,2,1,0:T(8,128)S(1)}, f32[5,2,16,128]{3,2,1,0:T(8,128)S(1)}, u32[]{:S(2)}, u32[]{:S(2)}) collective-permute-start(f32[5,2,16,128]{3,2,1,0:T(8,128)S(1)} %get-tuple-element.122), channel_id=1, source_target_pairs={{0,8},{8,16},{16,24},{1,9},{9,17},{17,25},{2,10},{10,18},{18,26},{... | collective-permute-start | bytes 245768 | tf_op jit(solution)/shard_map/ppermute | solution.py:19
  7.3 3.8 %collective-permute-done.1 = f32[5,2,16,128]{3,2,1,0:T(8,128)S(1)} collective-permute-done((f32[5,2,16,128]{3,2,1,0:T(8,128)S(1)}, f32[5,2,16,128]{3,2,1,0:T(8,128)S(1)}, u32[]{:S(2)}, u32[]{:S(2)}) %collective-permute-start.1) | collective-permute-done | bytes 81952 | tf_op jit(solution)/shard_map/ppermute | solution.py:20
  19.0 5.5 %reshape_broadcast_in_dim.3 = f32[4,2,8,2,64,2]{5,4,3,2,1,0:T(8,128)} reshape(f32[8,16,128]{2,1,0:T(8,128)S(1)} %copy-done.1) | data formatting | bytes 131072 | tf_op jit(solution)/shard_map/reshape;broadcast_in_dim | solution.py:43
  29.8 4.0 %collective-permute-start.5 = (f32[5,12,20,2]{2,3,1,0:T(2,128)S(1)}, f32[5,12,20,2]{2,3,1,0:T(2,128)S(1)}, u32[]{:S(2)}, u32[]{:S(2)}) collective-permute-start(f32[5,12,20,2]{2,3,1,0:T(2,128)S(1)} %copy.767), channel_id=1, source_target_pairs={{1,0},{2,1},{3,2},{5,4},{6,5},{7,6},{9,8},{10,9},{11,10},{13,12},{... | collective-permute-start | bytes 28808 | tf_op jit(solution)/shard_map/ppermute | solution.py:20
  33.8 38.6 %psum.14 = f32[4,4]{0,1:T(4,128)S(1)} all-reduce(f32[4,4]{0,1:T(4,128)S(1)} %convolution_bitcast_fusion.1), channel_id=1, replica_groups=mesh['gx'=4,'gy'=2,'gz'=4] {'gx','gy','gz'}, use_global_device_ids=true, to_apply=%region_0.0 | all-reduce | flops 16 | bytes 128 | tf_op jit(solution)/shard_map/psum | solution.py:134
  77.0 4.7 %copy.690 = f32[4,8,16,128]{0,3,2,1:T(8,128)} copy(f32[4,8,16,128]{3,2,1,0:T(8,128)S(1)} %fusion.35) | data formatting | bytes 524288 | tf_op jit(solution)/shard_map/sub | solution.py:112
  81.7 8.7 %reduce_sum.102 = f32[4,4,8,64]{0,3,2,1:T(8,128)S(1)} reduce(f32[4,4,2,8,2,64,2]{0,6,5,4,3,2,1:T(2,128)} %bitcast.130, f32[]{:T(128)} %constant.248.clone.1), dimensions={2,4,6}, to_apply=%region_4.0 | reduce | flops 57344 | bytes 294916 | tf_op jit(solution)/shard_map/reduce_sum | solution.py:43
  90.8 5.3 %collective-permute-start.6 = (f32[5,2,8,64]{3,2,1,0:T(8,128)S(1)}, f32[5,2,8,64]{3,2,1,0:T(8,128)S(1)}, u32[]{:S(2)}, u32[]{:S(2)}) collective-permute-start(f32[5,2,8,64]{3,2,1,0:T(8,128)S(1)} %get-tuple-element.154), channel_id=1, source_target_pairs={{0,8},{8,16},{16,24},{1,9},{9,17},{17,25},{2,10},{10,18},{18,26},{... | collective-permute-start | bytes 61448 | tf_op jit(solution)/shard_map/ppermute | solution.py:19
  109.4 4.0 %collective-permute-start.11 = (f32[5,8,12,2]{3,1,2,0:T(8,128)S(1)}, f32[5,8,12,2]{3,1,2,0:T(8,128)S(1)}, u32[]{:S(2)}, u32[]{:S(2)}) collective-permute-start(f32[5,8,12,2]{3,1,2,0:T(8,128)S(1)} %get-tuple-element.131), channel_id=1, source_target_pairs={{1,0},{2,1},{3,2},{5,4},{6,5},{7,6},{9,8},{10,9},{11,10},{13,12},{... | collective-permute-start | bytes 11528 | tf_op jit(solution)/shard_map/ppermute | solution.py:20
  126.0 38.6 %psum.15 = f32[4,4]{0,1:T(4,128)S(1)} all-reduce(f32[4,4]{0,1:T(4,128)S(1)} %convolution_bitcast_fusion), channel_id=1, replica_groups=mesh['gx'=4,'gy'=2,'gz'=4] {'gx','gy','gz'}, use_global_device_ids=true, to_apply=%region_1.0 | all-reduce | flops 16 | bytes 128 | tf_op jit(solution)/shard_map/psum | solution.py:137
  164.7 4.3 %collective-permute-start.14 = (f32[5,6,2,32]{3,2,1,0:T(2,128)S(1)}, f32[5,6,2,32]{3,2,1,0:T(2,128)S(1)}, u32[]{:S(2)}, u32[]{:S(2)}) collective-permute-start(f32[5,6,2,32]{3,2,1,0:T(2,128)S(1)} %get-tuple-element.158), channel_id=1, source_target_pairs={{0,4},{1,5},{2,6},{3,7},{8,12},{9,13},{10,14},{11,15},{16,20},{17,... | collective-permute-start | bytes 23048 | tf_op jit(solution)/shard_map/ppermute | solution.py:19
  175.1 4.0 %collective-permute-start.17 = (f32[5,6,8,2]{3,2,1,0:T(8,128)S(1)}, f32[5,6,8,2]{3,2,1,0:T(8,128)S(1)}, u32[]{:S(2)}, u32[]{:S(2)}) collective-permute-start(f32[5,6,8,2]{3,2,1,0:T(8,128)S(1)} %get-tuple-element.151), channel_id=1, source_target_pairs={{1,0},{2,1},{3,2},{5,4},{6,5},{7,6},{9,8},{10,9},{11,10},{13,12},{... | collective-permute-start | bytes 5768 | tf_op jit(solution)/shard_map/ppermute | solution.py:20
  181.9 61.1 %all-gather = f32[32,32,5]{1,2,0:T(8,128)S(1)} all-gather(f32[1,32,5]{1,2,0:T(8,128)S(1)} %maximum_bitcast_fusion), channel_id=1, replica_groups=mesh['gx'=4,'gy'=2,'gz'=4] {'gx','gy','gz'}, dimensions={0}, use_global_device_ids=true | all-gather | bytes 21120 | tf_op jit(solution)/shard_map/all_gather | solution.py:74
  247.3 8.6 %collective-permute-start.18 = (f32[4,1,4,32]{3,2,1,0:T(4,128)S(1)}, f32[4,1,4,32]{3,2,1,0:T(4,128)S(1)}, u32[]{:S(2)}, u32[]{:S(2)}) collective-permute-start(f32[4,1,4,32]{3,2,1,0:T(4,128)S(1)} %get-tuple-element.175), channel_id=1, source_target_pairs={{8,0},{16,8},{24,16},{9,1},{17,9},{25,17},{10,2},{18,10},{26,18},{... | collective-permute-start | bytes 6152 | tf_op jit(solution)/shard_map/ppermute | solution.py:20
  271.7 4.3 %collective-permute-done.23 = f32[4,4,6,1]{3,1,2,0:T(4,128)S(1)} collective-permute-done((f32[4,4,6,1]{3,1,2,0:T(4,128)S(1)}, f32[4,4,6,1]{3,1,2,0:T(4,128)S(1)}, u32[]{:S(2)}, u32[]{:S(2)}) %collective-permute-start.23) | collective-permute-done | bytes 416 | tf_op jit(solution)/shard_map/ppermute | solution.py:19
  279.6 5.3 %collective-permute-start.25 = (f32[4,1,8,64]{3,2,1,0:T(8,128)S(1)}, f32[4,1,8,64]{3,2,1,0:T(8,128)S(1)}, u32[]{:S(2)}, u32[]{:S(2)}) collective-permute-start(f32[4,1,8,64]{3,2,1,0:T(8,128)S(1)} %get-tuple-element.156), channel_id=1, source_target_pairs={{0,8},{8,16},{16,24},{1,9},{9,17},{17,25},{2,10},{10,18},{18,26},{... | collective-permute-start | bytes 24584 | tf_op jit(solution)/shard_map/ppermute | solution.py:19
  292.4 3.7 %collective-permute-start.28 = (f32[4,6,10,1]{3,0,2,1:T(4,128)S(1)}, f32[4,6,10,1]{3,0,2,1:T(4,128)S(1)}, u32[]{:S(2)}, u32[]{:S(2)}) collective-permute-start(f32[4,6,10,1]{3,0,2,1:T(4,128)S(1)} %get-tuple-element.146), channel_id=1, source_target_pairs={{1,0},{2,1},{3,2},{5,4},{6,5},{7,6},{9,8},{10,9},{11,10},{13,12},{... | collective-permute-start | bytes 2888 | tf_op jit(solution)/shard_map/ppermute | solution.py:20
  298.2 4.1 %collective-permute-done.29 = f32[4,6,10,1]{3,0,2,1:T(4,128)S(1)} collective-permute-done((f32[4,6,10,1]{3,0,2,1:T(4,128)S(1)}, f32[4,6,10,1]{3,0,2,1:T(4,128)S(1)}, u32[]{:S(2)}, u32[]{:S(2)}) %collective-permute-start.29) | collective-permute-done | bytes 992 | tf_op jit(solution)/shard_map/ppermute | solution.py:19
  309.8 6.7 %collective-permute-start.31 = (f32[4,1,16,128]{3,2,1,0:T(8,128)S(1)}, f32[4,1,16,128]{3,2,1,0:T(8,128)S(1)}, u32[]{:S(2)}, u32[]{:S(2)}) collective-permute-start(f32[4,1,16,128]{3,2,1,0:T(8,128)S(1)} %get-tuple-element.128), channel_id=1, source_target_pairs={{0,8},{8,16},{16,24},{1,9},{9,17},{17,25},{2,10},{10,18},{18,26},{... | collective-permute-start | bytes 98312 | tf_op jit(solution)/shard_map/ppermute | solution.py:19
  331.4 4.0 %collective-permute-done.34 = f32[4,10,18,1]{3,0,2,1:T(4,128)S(1)} collective-permute-done((f32[4,10,18,1]{3,0,2,1:T(4,128)S(1)}, f32[4,10,18,1]{3,0,2,1:T(4,128)S(1)}, u32[]{:S(2)}, u32[]{:S(2)}) %collective-permute-start.34) | collective-permute-done | bytes 2912 | tf_op jit(solution)/shard_map/ppermute | solution.py:20
  335.4 4.1 %collective-permute-done.35 = f32[4,10,18,1]{3,0,2,1:T(4,128)S(1)} collective-permute-done((f32[4,10,18,1]{3,0,2,1:T(4,128)S(1)}, f32[4,10,18,1]{3,0,2,1:T(4,128)S(1)}, u32[]{:S(2)}, u32[]{:S(2)}) %collective-permute-start.35) | collective-permute-done | bytes 2912 | tf_op jit(solution)/shard_map/ppermute | solution.py:19
  342.1 4.1 %collective-permute-start.37 = (f32[4,1,16,128]{3,2,1,0:T(8,128)S(1)}, f32[4,1,16,128]{3,2,1,0:T(8,128)S(1)}, u32[]{:S(2)}, u32[]{:S(2)}) collective-permute-start(f32[4,1,16,128]{3,2,1,0:T(8,128)S(1)} %get-tuple-element.126), channel_id=1, source_target_pairs={{0,8},{8,16},{16,24},{1,9},{9,17},{17,25},{2,10},{10,18},{18,26},{... | collective-permute-start | bytes 98312 | tf_op jit(solution)/shard_map/ppermute | solution.py:19
  359.5 4.7 %collective-permute-done.40 = f32[4,10,18,1]{3,0,2,1:T(4,128)S(1)} collective-permute-done((f32[4,10,18,1]{3,0,2,1:T(4,128)S(1)}, f32[4,10,18,1]{3,0,2,1:T(4,128)S(1)}, u32[]{:S(2)}, u32[]{:S(2)}) %collective-permute-start.40) | collective-permute-done | bytes 2912 | tf_op jit(solution)/shard_map/ppermute | solution.py:20
  364.2 4.4 %collective-permute-done.41 = f32[4,10,18,1]{3,0,2,1:T(4,128)S(1)} collective-permute-done((f32[4,10,18,1]{3,0,2,1:T(4,128)S(1)}, f32[4,10,18,1]{3,0,2,1:T(4,128)S(1)}, u32[]{:S(2)}, u32[]{:S(2)}) %collective-permute-start.41) | collective-permute-done | bytes 2912 | tf_op jit(solution)/shard_map/ppermute | solution.py:19
  (279 shorter events, 127.5 us)
Async XLA Ops:
  12.1 15.0 %collective-permute-start.2 = (f32[5,12,2,128]{3,2,1,0:T(2,128)S(1)}, f32[5,12,2,128]{3,2,1,0:T(2,128)S(1)}, u32[]{:S(2)}, u32[]{:S(2)}) collective-permute-start(f32[5,12,2,128]{3,2,1,0:T(2,128)S(1)} %get-tuple-element.108), channel_id=1, source_target_pairs={{0,4},{1,5},{2,6},{3,7},{8,12},{9,13},{10,14},{11,15},{16,20},{17,... | collective-permute-start | bytes 184328 | tf_op jit(solution)/shard_map/ppermute | solution.py:19
  15.3 11.9 %collective-permute-start.3 = (f32[5,12,2,128]{3,2,1,0:T(2,128)S(1)}, f32[5,12,2,128]{3,2,1,0:T(2,128)S(1)}, u32[]{:S(2)}, u32[]{:S(2)}) collective-permute-start(f32[5,12,2,128]{3,2,1,0:T(2,128)S(1)} %get-tuple-element.109), channel_id=1, source_target_pairs={{4,0},{5,1},{6,2},{7,3},{12,8},{13,9},{14,10},{15,11},{20,16},{21,... | collective-permute-start | bytes 184328 | tf_op jit(solution)/shard_map/ppermute | solution.py:20
  28.0 44.4 %collective-permute-start.4 = (f32[5,12,20,2]{2,3,1,0:T(2,128)S(1)}, f32[5,12,20,2]{2,3,1,0:T(2,128)S(1)}, u32[]{:S(2)}, u32[]{:S(2)}) collective-permute-start(f32[5,12,20,2]{2,3,1,0:T(2,128)S(1)} %copy.766), channel_id=1, source_target_pairs={{0,1},{1,2},{2,3},{4,5},{5,6},{6,7},{8,9},{9,10},{10,11},{12,13},{... | collective-permute-start | bytes 28808 | tf_op jit(solution)/shard_map/ppermute | solution.py:19
  29.8 43.1 %collective-permute-start.5 = (f32[5,12,20,2]{2,3,1,0:T(2,128)S(1)}, f32[5,12,20,2]{2,3,1,0:T(2,128)S(1)}, u32[]{:S(2)}, u32[]{:S(2)}) collective-permute-start(f32[5,12,20,2]{2,3,1,0:T(2,128)S(1)} %copy.767), channel_id=1, source_target_pairs={{1,0},{2,1},{3,2},{5,4},{6,5},{7,6},{9,8},{10,9},{11,10},{13,12},{... | collective-permute-start | bytes 28808 | tf_op jit(solution)/shard_map/ppermute | solution.py:20
  90.8 8.9 %collective-permute-start.6 = (f32[5,2,8,64]{3,2,1,0:T(8,128)S(1)}, f32[5,2,8,64]{3,2,1,0:T(8,128)S(1)}, u32[]{:S(2)}, u32[]{:S(2)}) collective-permute-start(f32[5,2,8,64]{3,2,1,0:T(8,128)S(1)} %get-tuple-element.154), channel_id=1, source_target_pairs={{0,8},{8,16},{16,24},{1,9},{9,17},{17,25},{2,10},{10,18},{18,26},{... | collective-permute-start | bytes 61448 | tf_op jit(solution)/shard_map/ppermute | solution.py:19
  108.1 9.3 %collective-permute-start.10 = (f32[5,8,12,2]{3,1,2,0:T(8,128)S(1)}, f32[5,8,12,2]{3,1,2,0:T(8,128)S(1)}, u32[]{:S(2)}, u32[]{:S(2)}) collective-permute-start(f32[5,8,12,2]{3,1,2,0:T(8,128)S(1)} %get-tuple-element.130), channel_id=1, source_target_pairs={{0,1},{1,2},{2,3},{4,5},{5,6},{6,7},{8,9},{9,10},{10,11},{12,13},{... | collective-permute-start | bytes 11528 | tf_op jit(solution)/shard_map/ppermute | solution.py:19
  109.4 9.7 %collective-permute-start.11 = (f32[5,8,12,2]{3,1,2,0:T(8,128)S(1)}, f32[5,8,12,2]{3,1,2,0:T(8,128)S(1)}, u32[]{:S(2)}, u32[]{:S(2)}) collective-permute-start(f32[5,8,12,2]{3,1,2,0:T(8,128)S(1)} %get-tuple-element.131), channel_id=1, source_target_pairs={{1,0},{2,1},{3,2},{5,4},{6,5},{7,6},{9,8},{10,9},{11,10},{13,12},{... | collective-permute-start | bytes 11528 | tf_op jit(solution)/shard_map/ppermute | solution.py:20
  121.7 42.9 %collective-permute-start.12 = (f32[5,2,4,32]{3,2,1,0:T(4,128)S(1)}, f32[5,2,4,32]{3,2,1,0:T(4,128)S(1)}, u32[]{:S(2)}, u32[]{:S(2)}) collective-permute-start(f32[5,2,4,32]{3,2,1,0:T(4,128)S(1)} %pad_maximum_fusion.50), channel_id=1, source_target_pairs={{0,8},{8,16},{16,24},{1,9},{9,17},{17,25},{2,10},{10,18},{18,26},{... | collective-permute-start | bytes 15368 | tf_op jit(solution)/shard_map/ppermute | solution.py:19
  123.6 41.0 %collective-permute-start.13 = (f32[5,2,4,32]{3,2,1,0:T(4,128)S(1)}, f32[5,2,4,32]{3,2,1,0:T(4,128)S(1)}, u32[]{:S(2)}, u32[]{:S(2)}) collective-permute-start(f32[5,2,4,32]{3,2,1,0:T(4,128)S(1)} %pad_maximum_fusion.50), channel_id=1, source_target_pairs={{8,0},{16,8},{24,16},{9,1},{17,9},{25,17},{10,2},{18,10},{26,18},{... | collective-permute-start | bytes 15368 | tf_op jit(solution)/shard_map/ppermute | solution.py:20
  164.7 5.8 %collective-permute-start.14 = (f32[5,6,2,32]{3,2,1,0:T(2,128)S(1)}, f32[5,6,2,32]{3,2,1,0:T(2,128)S(1)}, u32[]{:S(2)}, u32[]{:S(2)}) collective-permute-start(f32[5,6,2,32]{3,2,1,0:T(2,128)S(1)} %get-tuple-element.158), channel_id=1, source_target_pairs={{0,4},{1,5},{2,6},{3,7},{8,12},{9,13},{10,14},{11,15},{16,20},{17,... | collective-permute-start | bytes 23048 | tf_op jit(solution)/shard_map/ppermute | solution.py:19
  175.1 5.8 %collective-permute-start.17 = (f32[5,6,8,2]{3,2,1,0:T(8,128)S(1)}, f32[5,6,8,2]{3,2,1,0:T(8,128)S(1)}, u32[]{:S(2)}, u32[]{:S(2)}) collective-permute-start(f32[5,6,8,2]{3,2,1,0:T(8,128)S(1)} %get-tuple-element.151), channel_id=1, source_target_pairs={{1,0},{2,1},{3,2},{5,4},{6,5},{7,6},{9,8},{10,9},{11,10},{13,12},{... | collective-permute-start | bytes 5768 | tf_op jit(solution)/shard_map/ppermute | solution.py:20
  247.3 12.6 %collective-permute-start.18 = (f32[4,1,4,32]{3,2,1,0:T(4,128)S(1)}, f32[4,1,4,32]{3,2,1,0:T(4,128)S(1)}, u32[]{:S(2)}, u32[]{:S(2)}) collective-permute-start(f32[4,1,4,32]{3,2,1,0:T(4,128)S(1)} %get-tuple-element.175), channel_id=1, source_target_pairs={{8,0},{16,8},{24,16},{9,1},{17,9},{25,17},{10,2},{18,10},{26,18},{... | collective-permute-start | bytes 6152 | tf_op jit(solution)/shard_map/ppermute | solution.py:20
  269.7 6.2 %collective-permute-start.23 = (f32[4,4,6,1]{3,1,2,0:T(4,128)S(1)}, f32[4,4,6,1]{3,1,2,0:T(4,128)S(1)}, u32[]{:S(2)}, u32[]{:S(2)}) collective-permute-start(f32[4,4,6,1]{3,1,2,0:T(4,128)S(1)} %get-tuple-element.163), channel_id=1, source_target_pairs={{0,1},{1,2},{2,3},{4,5},{5,6},{6,7},{8,9},{9,10},{10,11},{12,13},{... | collective-permute-start | bytes 1160 | tf_op jit(solution)/shard_map/ppermute | solution.py:19
  276.8 8.8 %collective-permute-start.24 = (f32[4,1,8,64]{3,2,1,0:T(8,128)S(1)}, f32[4,1,8,64]{3,2,1,0:T(8,128)S(1)}, u32[]{:S(2)}, u32[]{:S(2)}) collective-permute-start(f32[4,1,8,64]{3,2,1,0:T(8,128)S(1)} %get-tuple-element.157), channel_id=1, source_target_pairs={{8,0},{16,8},{24,16},{9,1},{17,9},{25,17},{10,2},{18,10},{26,18},{... | collective-permute-start | bytes 24584 | tf_op jit(solution)/shard_map/ppermute | solution.py:20
  279.6 6.1 %collective-permute-start.25 = (f32[4,1,8,64]{3,2,1,0:T(8,128)S(1)}, f32[4,1,8,64]{3,2,1,0:T(8,128)S(1)}, u32[]{:S(2)}, u32[]{:S(2)}) collective-permute-start(f32[4,1,8,64]{3,2,1,0:T(8,128)S(1)} %get-tuple-element.156), channel_id=1, source_target_pairs={{0,8},{8,16},{16,24},{1,9},{9,17},{17,25},{2,10},{10,18},{18,26},{... | collective-permute-start | bytes 24584 | tf_op jit(solution)/shard_map/ppermute | solution.py:19
  292.4 5.8 %collective-permute-start.28 = (f32[4,6,10,1]{3,0,2,1:T(4,128)S(1)}, f32[4,6,10,1]{3,0,2,1:T(4,128)S(1)}, u32[]{:S(2)}, u32[]{:S(2)}) collective-permute-start(f32[4,6,10,1]{3,0,2,1:T(4,128)S(1)} %get-tuple-element.146), channel_id=1, source_target_pairs={{1,0},{2,1},{3,2},{5,4},{6,5},{7,6},{9,8},{10,9},{11,10},{13,12},{... | collective-permute-start | bytes 2888 | tf_op jit(solution)/shard_map/ppermute | solution.py:20
  296.1 6.2 %collective-permute-start.29 = (f32[4,6,10,1]{3,0,2,1:T(4,128)S(1)}, f32[4,6,10,1]{3,0,2,1:T(4,128)S(1)}, u32[]{:S(2)}, u32[]{:S(2)}) collective-permute-start(f32[4,6,10,1]{3,0,2,1:T(4,128)S(1)} %get-tuple-element.147), channel_id=1, source_target_pairs={{0,1},{1,2},{2,3},{4,5},{5,6},{6,7},{8,9},{9,10},{10,11},{12,13},{... | collective-permute-start | bytes 2888 | tf_op jit(solution)/shard_map/ppermute | solution.py:19
  307.8 10.6 %collective-permute-start.30 = (f32[4,1,16,128]{3,2,1,0:T(8,128)S(1)}, f32[4,1,16,128]{3,2,1,0:T(8,128)S(1)}, u32[]{:S(2)}, u32[]{:S(2)}) collective-permute-start(f32[4,1,16,128]{3,2,1,0:T(8,128)S(1)} %get-tuple-element.129), channel_id=1, source_target_pairs={{8,0},{16,8},{24,16},{9,1},{17,9},{25,17},{10,2},{18,10},{26,18},{... | collective-permute-start | bytes 98312 | tf_op jit(solution)/shard_map/ppermute | solution.py:20
  309.8 8.7 %collective-permute-start.31 = (f32[4,1,16,128]{3,2,1,0:T(8,128)S(1)}, f32[4,1,16,128]{3,2,1,0:T(8,128)S(1)}, u32[]{:S(2)}, u32[]{:S(2)}) collective-permute-start(f32[4,1,16,128]{3,2,1,0:T(8,128)S(1)} %get-tuple-element.128), channel_id=1, source_target_pairs={{0,8},{8,16},{16,24},{1,9},{9,17},{17,25},{2,10},{10,18},{18,26},{... | collective-permute-start | bytes 98312 | tf_op jit(solution)/shard_map/ppermute | solution.py:19
  325.5 9.9 %collective-permute-start.34 = (f32[4,10,18,1]{3,0,2,1:T(4,128)S(1)}, f32[4,10,18,1]{3,0,2,1:T(4,128)S(1)}, u32[]{:S(2)}, u32[]{:S(2)}) collective-permute-start(f32[4,10,18,1]{3,0,2,1:T(4,128)S(1)} %get-tuple-element.116), channel_id=1, source_target_pairs={{1,0},{2,1},{3,2},{5,4},{6,5},{7,6},{9,8},{10,9},{11,10},{13,12},{... | collective-permute-start | bytes 8648 | tf_op jit(solution)/shard_map/ppermute | solution.py:20
  329.2 10.3 %collective-permute-start.35 = (f32[4,10,18,1]{3,0,2,1:T(4,128)S(1)}, f32[4,10,18,1]{3,0,2,1:T(4,128)S(1)}, u32[]{:S(2)}, u32[]{:S(2)}) collective-permute-start(f32[4,10,18,1]{3,0,2,1:T(4,128)S(1)} %get-tuple-element.117), channel_id=1, source_target_pairs={{0,1},{1,2},{2,3},{4,5},{5,6},{6,7},{8,9},{9,10},{10,11},{12,13},{... | collective-permute-start | bytes 8648 | tf_op jit(solution)/shard_map/ppermute | solution.py:19
  340.2 6.6 %collective-permute-start.36 = (f32[4,1,16,128]{3,2,1,0:T(8,128)S(1)}, f32[4,1,16,128]{3,2,1,0:T(8,128)S(1)}, u32[]{:S(2)}, u32[]{:S(2)}) collective-permute-start(f32[4,1,16,128]{3,2,1,0:T(8,128)S(1)} %get-tuple-element.127), channel_id=1, source_target_pairs={{8,0},{16,8},{24,16},{9,1},{17,9},{25,17},{10,2},{18,10},{26,18},{... | collective-permute-start | bytes 98312 | tf_op jit(solution)/shard_map/ppermute | solution.py:20
  354.2 10.0 %collective-permute-start.40 = (f32[4,10,18,1]{3,0,2,1:T(4,128)S(1)}, f32[4,10,18,1]{3,0,2,1:T(4,128)S(1)}, u32[]{:S(2)}, u32[]{:S(2)}) collective-permute-start(f32[4,10,18,1]{3,0,2,1:T(4,128)S(1)} %get-tuple-element.112), channel_id=1, source_target_pairs={{1,0},{2,1},{3,2},{5,4},{6,5},{7,6},{9,8},{10,9},{11,10},{13,12},{... | collective-permute-start | bytes 8648 | tf_op jit(solution)/shard_map/ppermute | solution.py:20
  356.1 12.5 %collective-permute-start.41 = (f32[4,10,18,1]{3,0,2,1:T(4,128)S(1)}, f32[4,10,18,1]{3,0,2,1:T(4,128)S(1)}, u32[]{:S(2)}, u32[]{:S(2)}) collective-permute-start(f32[4,10,18,1]{3,0,2,1:T(4,128)S(1)} %get-tuple-element.113), channel_id=1, source_target_pairs={{0,1},{1,2},{2,3},{4,5},{5,6},{6,7},{8,9},{9,10},{10,11},{12,13},{... | collective-permute-start | bytes 8648 | tf_op jit(solution)/shard_map/ppermute | solution.py:19
  (25 other events, 175.3 us)
where the time goes:
time: 371 us; the launch traced here: 370 us
  blocking collectives  138 us (37%)
  starting transfers between devices  110 us (30%)
  waiting for transfers between devices  57.7 us (16%)
  other arithmetic  29.1 us (8%)
  local copies, waits for them, and re-layouts  26.4 us (7%)
  matrix products  6.55 us (2%)
    all_gather x1, blocking collectives, agglomerate(): gathered = lax.all_gather(flattened, ('gx', 'gy', 'gz'), axis=1, tiled=True)  61.1 us
    ppermute x21, starting transfers between devices, with_halo(): before = lax.ppermute(last, axis, up)  56.1 us
    ppermute x21, starting transfers between devices, with_halo(): after = lax.ppermute(leading, axis, down)  53.7 us
    psum x1, blocking collectives, per_device(): projection = lax.psum(basis_local, ('gx', 'gy', 'gz')) / total_cells  38.6 us
    psum x1, blocking collectives, per_device(): gram = lax.psum(gram_local, ('gx', 'gy', 'gz')) / total_cells  38.6 us
    ppermute x21, waiting for transfers between devices, with_halo(): after = lax.ppermute(leading, axis, down)  36.8 us
    ppermute x21, waiting for transfers between devices, with_halo(): before = lax.ppermute(last, axis, up)  20.8 us
    reduce_sum x14, other arithmetic, restrict(): field.reshape(depth, size_a // 2, 2, size_b // 2, 2, size_c // 2, 2)  13 us
  transfers between devices with their start and end apart: 42, of which 22 were waited for; matrix products, arithmetic and copies ran while one was open for 7% of the time, Pallas kernels for 0%

commit v1 on v0

--- a/solution.py
+++ b/solution.py
@@ -71,7 +71,7 @@
     stacked = jnp.concatenate([source, coeffs[None]], axis=0)
     depth, size_a, size_b, size_c = stacked.shape
     flattened = stacked.reshape(depth, size_a * size_b * size_c)
-    gathered = lax.all_gather(flattened, ("gx", "gy", "gz"), axis=1, tiled=True)
+    gathered = jnp.concatenate(lax.all_gather(flattened, ("gx", "gy", "gz")), axis=1)
     count_x, count_y, count_z = (lax.axis_size("gx"), lax.axis_size("gy"), lax.axis_size("gz"))
     gathered = gathered.reshape(depth, count_x, count_y, count_z, size_a, size_b, size_c)
     gathered = gathered.transpose(0, 1, 4, 2, 5, 3, 6).reshape(

time: 371 us -> 371 us (level)
  no operation moved by 1% of the time
where the time goes in v1:
time: 371 us; the launch traced here: 370 us
  blocking collectives  138 us (37%)
  starting transfers between devices  110 us (30%)
  waiting for transfers between devices  57.7 us (16%)
  other arithmetic  29.1 us (8%)
  local copies, waits for them, and re-layouts  26.4 us (7%)
  matrix products  6.54 us (2%)
    all_gather x1, blocking collectives, agglomerate(): lax.all_gather(flattened, ('gx', 'gy', 'gz'))  61.1 us
    ppermute x21, starting transfers between devices, with_halo(): before = lax.ppermute(last, axis, up)  55.9 us
    ppermute x21, starting transfers between devices, with_halo(): after = lax.ppermute(leading, axis, down)  53.7 us
    psum x1, blocking collectives, per_device(): projection = lax.psum(basis_local, ('gx', 'gy', 'gz')) / total_cells  38.6 us
    psum x1, blocking collectives, per_device(): gram = lax.psum(gram_local, ('gx', 'gy', 'gz')) / total_cells  38.6 us
    ppermute x21, waiting for transfers between devices, with_halo(): after = lax.ppermute(leading, axis, down)  36.8 us
    ppermute x21, waiting for transfers between devices, with_halo(): before = lax.ppermute(last, axis, up)  20.8 us
    reduce_sum x14, other arithmetic, restrict(): field.reshape(depth, size_a // 2, 2, size_b // 2, 2, size_c // 2, 2)  13 us
  transfers between devices with their start and end apart: 42, of which 22 were waited for; matrix products, arithmetic and copies ran while one was open for 7% of the time, Pallas kernels for 0%

profile of v1, /device:TPU:25, one launch (start us, length us, event | category | flops | bytes accessed | tf_op | source)
XLA Modules:
  0.0 369.7 jit_solution(18117572034051456794)
XLA Ops:
  1.6 3.7 %collective-permute-start = (f32[5,2,16,128]{3,2,1,0:T(8,128)S(1)}, f32[5,2,16,128]{3,2,1,0:T(8,128)S(1)}, u32[]{:S(2)}, u32[]{:S(2)}) collective-permute-start(f32[5,2,16,128]{3,2,1,0:T(8,128)S(1)} %get-tuple-element.122), channel_id=1, source_target_pairs={{0,8},{8,16},{16,24},{1,9},{9,17},{17,25},{2,10},{10,18},{18,26},{... | collective-permute-start | bytes 245768 | tf_op jit(solution)/shard_map/ppermute | solution.py:19
  7.3 3.8 %collective-permute-done.1 = f32[5,2,16,128]{3,2,1,0:T(8,128)S(1)} collective-permute-done((f32[5,2,16,128]{3,2,1,0:T(8,128)S(1)}, f32[5,2,16,128]{3,2,1,0:T(8,128)S(1)}, u32[]{:S(2)}, u32[]{:S(2)}) %collective-permute-start.1) | collective-permute-done | bytes 81952 | tf_op jit(solution)/shard_map/ppermute | solution.py:20
  19.0 5.5 %reshape_broadcast_in_dim.3 = f32[4,2,8,2,64,2]{5,4,3,2,1,0:T(8,128)} reshape(f32[8,16,128]{2,1,0:T(8,128)S(1)} %copy-done.1) | data formatting | bytes 131072 | tf_op jit(solution)/shard_map/reshape;broadcast_in_dim | solution.py:43
  29.8 4.0 %collective-permute-start.5 = (f32[5,12,20,2]{2,3,1,0:T(2,128)S(1)}, f32[5,12,20,2]{2,3,1,0:T(2,128)S(1)}, u32[]{:S(2)}, u32[]{:S(2)}) collective-permute-start(f32[5,12,20,2]{2,3,1,0:T(2,128)S(1)} %copy.774), channel_id=1, source_target_pairs={{1,0},{2,1},{3,2},{5,4},{6,5},{7,6},{9,8},{10,9},{11,10},{13,12},{... | collective-permute-start | bytes 28808 | tf_op jit(solution)/shard_map/ppermute | solution.py:20
  33.8 38.6 %psum.14 = f32[4,4]{0,1:T(4,128)S(1)} all-reduce(f32[4,4]{0,1:T(4,128)S(1)} %convolution_bitcast_fusion.1), channel_id=1, replica_groups=mesh['gx'=4,'gy'=2,'gz'=4] {'gx','gy','gz'}, use_global_device_ids=true, to_apply=%region_0.0 | all-reduce | flops 16 | bytes 128 | tf_op jit(solution)/shard_map/psum | solution.py:134
  77.0 4.7 %copy.695 = f32[4,8,16,128]{0,3,2,1:T(8,128)} copy(f32[4,8,16,128]{3,2,1,0:T(8,128)S(1)} %fusion.35) | data formatting | bytes 524288 | tf_op jit(solution)/shard_map/sub | solution.py:112
  81.7 8.7 %reduce_sum.102 = f32[4,4,8,64]{0,3,2,1:T(8,128)S(1)} reduce(f32[4,4,2,8,2,64,2]{0,6,5,4,3,2,1:T(2,128)} %bitcast.126, f32[]{:T(128)} %constant.248.clone.1), dimensions={2,4,6}, to_apply=%region_4.0 | reduce | flops 57344 | bytes 294916 | tf_op jit(solution)/shard_map/reduce_sum | solution.py:43
  90.8 5.3 %collective-permute-start.6 = (f32[5,2,8,64]{3,2,1,0:T(8,128)S(1)}, f32[5,2,8,64]{3,2,1,0:T(8,128)S(1)}, u32[]{:S(2)}, u32[]{:S(2)}) collective-permute-start(f32[5,2,8,64]{3,2,1,0:T(8,128)S(1)} %get-tuple-element.154), channel_id=1, source_target_pairs={{0,8},{8,16},{16,24},{1,9},{9,17},{17,25},{2,10},{10,18},{18,26},{... | collective-permute-start | bytes 61448 | tf_op jit(solution)/shard_map/ppermute | solution.py:19
  109.4 4.0 %collective-permute-start.11 = (f32[5,8,12,2]{3,1,2,0:T(8,128)S(1)}, f32[5,8,12,2]{3,1,2,0:T(8,128)S(1)}, u32[]{:S(2)}, u32[]{:S(2)}) collective-permute-start(f32[5,8,12,2]{3,1,2,0:T(8,128)S(1)} %get-tuple-element.131), channel_id=1, source_target_pairs={{1,0},{2,1},{3,2},{5,4},{6,5},{7,6},{9,8},{10,9},{11,10},{13,12},{... | collective-permute-start | bytes 11528 | tf_op jit(solution)/shard_map/ppermute | solution.py:20
  126.0 38.6 %psum.15 = f32[4,4]{0,1:T(4,128)S(1)} all-reduce(f32[4,4]{0,1:T(4,128)S(1)} %convolution_bitcast_fusion), channel_id=1, replica_groups=mesh['gx'=4,'gy'=2,'gz'=4] {'gx','gy','gz'}, use_global_device_ids=true, to_apply=%region_1.0 | all-reduce | flops 16 | bytes 128 | tf_op jit(solution)/shard_map/psum | solution.py:137
  164.7 4.3 %collective-permute-start.14 = (f32[5,6,2,32]{3,2,1,0:T(2,128)S(1)}, f32[5,6,2,32]{3,2,1,0:T(2,128)S(1)}, u32[]{:S(2)}, u32[]{:S(2)}) collective-permute-start(f32[5,6,2,32]{3,2,1,0:T(2,128)S(1)} %get-tuple-element.158), channel_id=1, source_target_pairs={{0,4},{1,5},{2,6},{3,7},{8,12},{9,13},{10,14},{11,15},{16,20},{17,... | collective-permute-start | bytes 23048 | tf_op jit(solution)/shard_map/ppermute | solution.py:19
  175.1 4.0 %collective-permute-start.17 = (f32[5,6,8,2]{3,2,1,0:T(8,128)S(1)}, f32[5,6,8,2]{3,2,1,0:T(8,128)S(1)}, u32[]{:S(2)}, u32[]{:S(2)}) collective-permute-start(f32[5,6,8,2]{3,2,1,0:T(8,128)S(1)} %get-tuple-element.151), channel_id=1, source_target_pairs={{1,0},{2,1},{3,2},{5,4},{6,5},{7,6},{9,8},{10,9},{11,10},{13,12},{... | collective-permute-start | bytes 5768 | tf_op jit(solution)/shard_map/ppermute | solution.py:20
  181.9 61.1 %all_gather.3 = f32[32,5,32]{2,1,0:T(8,128)S(1)} all-gather(f32[1,5,32]{2,1,0:T(8,128)S(1)} %pad_maximum_fusion.65), channel_id=1, replica_groups=mesh['gx'=4,'gy'=2,'gz'=4] {'gx','gy','gz'}, dimensions={0}, use_global_device_ids=true | all-gather | bytes 21120 | tf_op jit(solution)/shard_map/all_gather | solution.py:74
  247.1 8.6 %collective-permute-start.18 = (f32[4,1,4,32]{3,2,1,0:T(4,128)S(1)}, f32[4,1,4,32]{3,2,1,0:T(4,128)S(1)}, u32[]{:S(2)}, u32[]{:S(2)}) collective-permute-start(f32[4,1,4,32]{3,2,1,0:T(4,128)S(1)} %get-tuple-element.175), channel_id=1, source_target_pairs={{8,0},{16,8},{24,16},{9,1},{17,9},{25,17},{10,2},{18,10},{26,18},{... | collective-permute-start | bytes 6152 | tf_op jit(solution)/shard_map/ppermute | solution.py:20
  271.5 4.3 %collective-permute-done.23 = f32[4,4,6,1]{3,1,2,0:T(4,128)S(1)} collective-permute-done((f32[4,4,6,1]{3,1,2,0:T(4,128)S(1)}, f32[4,4,6,1]{3,1,2,0:T(4,128)S(1)}, u32[]{:S(2)}, u32[]{:S(2)}) %collective-permute-start.23) | collective-permute-done | bytes 416 | tf_op jit(solution)/shard_map/ppermute | solution.py:19
  279.4 5.3 %collective-permute-start.25 = (f32[4,1,8,64]{3,2,1,0:T(8,128)S(1)}, f32[4,1,8,64]{3,2,1,0:T(8,128)S(1)}, u32[]{:S(2)}, u32[]{:S(2)}) collective-permute-start(f32[4,1,8,64]{3,2,1,0:T(8,128)S(1)} %get-tuple-element.156), channel_id=1, source_target_pairs={{0,8},{8,16},{16,24},{1,9},{9,17},{17,25},{2,10},{10,18},{18,26},{... | collective-permute-start | bytes 24584 | tf_op jit(solution)/shard_map/ppermute | solution.py:19
  292.2 3.7 %collective-permute-start.28 = (f32[4,6,10,1]{3,0,2,1:T(4,128)S(1)}, f32[4,6,10,1]{3,0,2,1:T(4,128)S(1)}, u32[]{:S(2)}, u32[]{:S(2)}) collective-permute-start(f32[4,6,10,1]{3,0,2,1:T(4,128)S(1)} %get-tuple-element.146), channel_id=1, source_target_pairs={{1,0},{2,1},{3,2},{5,4},{6,5},{7,6},{9,8},{10,9},{11,10},{13,12},{... | collective-permute-start | bytes 2888 | tf_op jit(solution)/shard_map/ppermute | solution.py:20
  298.0 4.1 %collective-permute-done.29 = f32[4,6,10,1]{3,0,2,1:T(4,128)S(1)} collective-permute-done((f32[4,6,10,1]{3,0,2,1:T(4,128)S(1)}, f32[4,6,10,1]{3,0,2,1:T(4,128)S(1)}, u32[]{:S(2)}, u32[]{:S(2)}) %collective-permute-start.29) | collective-permute-done | bytes 992 | tf_op jit(solution)/shard_map/ppermute | solution.py:19
  309.5 6.5 %collective-permute-start.31 = (f32[4,1,16,128]{3,2,1,0:T(8,128)S(1)}, f32[4,1,16,128]{3,2,1,0:T(8,128)S(1)}, u32[]{:S(2)}, u32[]{:S(2)}) collective-permute-start(f32[4,1,16,128]{3,2,1,0:T(8,128)S(1)} %get-tuple-element.128), channel_id=1, source_target_pairs={{0,8},{8,16},{16,24},{1,9},{9,17},{17,25},{2,10},{10,18},{18,26},{... | collective-permute-start | bytes 98312 | tf_op jit(solution)/shard_map/ppermute | solution.py:19
  331.1 4.0 %collective-permute-done.34 = f32[4,10,18,1]{3,0,2,1:T(4,128)S(1)} collective-permute-done((f32[4,10,18,1]{3,0,2,1:T(4,128)S(1)}, f32[4,10,18,1]{3,0,2,1:T(4,128)S(1)}, u32[]{:S(2)}, u32[]{:S(2)}) %collective-permute-start.34) | collective-permute-done | bytes 2912 | tf_op jit(solution)/shard_map/ppermute | solution.py:20
  335.2 4.1 %collective-permute-done.35 = f32[4,10,18,1]{3,0,2,1:T(4,128)S(1)} collective-permute-done((f32[4,10,18,1]{3,0,2,1:T(4,128)S(1)}, f32[4,10,18,1]{3,0,2,1:T(4,128)S(1)}, u32[]{:S(2)}, u32[]{:S(2)}) %collective-permute-start.35) | collective-permute-done | bytes 2912 | tf_op jit(solution)/shard_map/ppermute | solution.py:19
  341.9 3.8 %collective-permute-start.37 = (f32[4,1,16,128]{3,2,1,0:T(8,128)S(1)}, f32[4,1,16,128]{3,2,1,0:T(8,128)S(1)}, u32[]{:S(2)}, u32[]{:S(2)}) collective-permute-start(f32[4,1,16,128]{3,2,1,0:T(8,128)S(1)} %get-tuple-element.126), channel_id=1, source_target_pairs={{0,8},{8,16},{16,24},{1,9},{9,17},{17,25},{2,10},{10,18},{18,26},{... | collective-permute-start | bytes 98312 | tf_op jit(solution)/shard_map/ppermute | solution.py:19
  359.3 4.7 %collective-permute-done.40 = f32[4,10,18,1]{3,0,2,1:T(4,128)S(1)} collective-permute-done((f32[4,10,18,1]{3,0,2,1:T(4,128)S(1)}, f32[4,10,18,1]{3,0,2,1:T(4,128)S(1)}, u32[]{:S(2)}, u32[]{:S(2)}) %collective-permute-start.40) | collective-permute-done | bytes 2912 | tf_op jit(solution)/shard_map/ppermute | solution.py:20
  364.0 4.4 %collective-permute-done.41 = f32[4,10,18,1]{3,0,2,1:T(4,128)S(1)} collective-permute-done((f32[4,10,18,1]{3,0,2,1:T(4,128)S(1)}, f32[4,10,18,1]{3,0,2,1:T(4,128)S(1)}, u32[]{:S(2)}, u32[]{:S(2)}) %collective-permute-start.41) | collective-permute-done | bytes 2912 | tf_op jit(solution)/shard_map/ppermute | solution.py:19
  (277 shorter events, 127.7 us)
Async XLA Ops:
  12.1 15.0 %collective-permute-start.2 = (f32[5,12,2,128]{3,2,1,0:T(2,128)S(1)}, f32[5,12,2,128]{3,2,1,0:T(2,128)S(1)}, u32[]{:S(2)}, u32[]{:S(2)}) collective-permute-start(f32[5,12,2,128]{3,2,1,0:T(2,128)S(1)} %get-tuple-element.108), channel_id=1, source_target_pairs={{0,4},{1,5},{2,6},{3,7},{8,12},{9,13},{10,14},{11,15},{16,20},{17,... | collective-permute-start | bytes 184328 | tf_op jit(solution)/shard_map/ppermute | solution.py:19
  15.3 11.9 %collective-permute-start.3 = (f32[5,12,2,128]{3,2,1,0:T(2,128)S(1)}, f32[5,12,2,128]{3,2,1,0:T(2,128)S(1)}, u32[]{:S(2)}, u32[]{:S(2)}) collective-permute-start(f32[5,12,2,128]{3,2,1,0:T(2,128)S(1)} %get-tuple-element.109), channel_id=1, source_target_pairs={{4,0},{5,1},{6,2},{7,3},{12,8},{13,9},{14,10},{15,11},{20,16},{21,... | collective-permute-start | bytes 184328 | tf_op jit(solution)/shard_map/ppermute | solution.py:20
  28.0 44.4 %collective-permute-start.4 = (f32[5,12,20,2]{2,3,1,0:T(2,128)S(1)}, f32[5,12,20,2]{2,3,1,0:T(2,128)S(1)}, u32[]{:S(2)}, u32[]{:S(2)}) collective-permute-start(f32[5,12,20,2]{2,3,1,0:T(2,128)S(1)} %copy.773), channel_id=1, source_target_pairs={{0,1},{1,2},{2,3},{4,5},{5,6},{6,7},{8,9},{9,10},{10,11},{12,13},{... | collective-permute-start | bytes 28808 | tf_op jit(solution)/shard_map/ppermute | solution.py:19
  29.8 43.1 %collective-permute-start.5 = (f32[5,12,20,2]{2,3,1,0:T(2,128)S(1)}, f32[5,12,20,2]{2,3,1,0:T(2,128)S(1)}, u32[]{:S(2)}, u32[]{:S(2)}) collective-permute-start(f32[5,12,20,2]{2,3,1,0:T(2,128)S(1)} %copy.774), channel_id=1, source_target_pairs={{1,0},{2,1},{3,2},{5,4},{6,5},{7,6},{9,8},{10,9},{11,10},{13,12},{... | collective-permute-start | bytes 28808 | tf_op jit(solution)/shard_map/ppermute | solution.py:20
  90.8 8.9 %collective-permute-start.6 = (f32[5,2,8,64]{3,2,1,0:T(8,128)S(1)}, f32[5,2,8,64]{3,2,1,0:T(8,128)S(1)}, u32[]{:S(2)}, u32[]{:S(2)}) collective-permute-start(f32[5,2,8,64]{3,2,1,0:T(8,128)S(1)} %get-tuple-element.154), channel_id=1, source_target_pairs={{0,8},{8,16},{16,24},{1,9},{9,17},{17,25},{2,10},{10,18},{18,26},{... | collective-permute-start | bytes 61448 | tf_op jit(solution)/shard_map/ppermute | solution.py:19
  108.1 9.3 %collective-permute-start.10 = (f32[5,8,12,2]{3,1,2,0:T(8,128)S(1)}, f32[5,8,12,2]{3,1,2,0:T(8,128)S(1)}, u32[]{:S(2)}, u32[]{:S(2)}) collective-permute-start(f32[5,8,12,2]{3,1,2,0:T(8,128)S(1)} %get-tuple-element.130), channel_id=1, source_target_pairs={{0,1},{1,2},{2,3},{4,5},{5,6},{6,7},{8,9},{9,10},{10,11},{12,13},{... | collective-permute-start | bytes 11528 | tf_op jit(solution)/shard_map/ppermute | solution.py:19
  109.4 9.7 %collective-permute-start.11 = (f32[5,8,12,2]{3,1,2,0:T(8,128)S(1)}, f32[5,8,12,2]{3,1,2,0:T(8,128)S(1)}, u32[]{:S(2)}, u32[]{:S(2)}) collective-permute-start(f32[5,8,12,2]{3,1,2,0:T(8,128)S(1)} %get-tuple-element.131), channel_id=1, source_target_pairs={{1,0},{2,1},{3,2},{5,4},{6,5},{7,6},{9,8},{10,9},{11,10},{13,12},{... | collective-permute-start | bytes 11528 | tf_op jit(solution)/shard_map/ppermute | solution.py:20
  121.7 42.9 %collective-permute-start.12 = (f32[5,2,4,32]{3,2,1,0:T(4,128)S(1)}, f32[5,2,4,32]{3,2,1,0:T(4,128)S(1)}, u32[]{:S(2)}, u32[]{:S(2)}) collective-permute-start(f32[5,2,4,32]{3,2,1,0:T(4,128)S(1)} %pad_maximum_fusion.50), channel_id=1, source_target_pairs={{0,8},{8,16},{16,24},{1,9},{9,17},{17,25},{2,10},{10,18},{18,26},{... | collective-permute-start | bytes 15368 | tf_op jit(solution)/shard_map/ppermute | solution.py:19
  123.6 41.0 %collective-permute-start.13 = (f32[5,2,4,32]{3,2,1,0:T(4,128)S(1)}, f32[5,2,4,32]{3,2,1,0:T(4,128)S(1)}, u32[]{:S(2)}, u32[]{:S(2)}) collective-permute-start(f32[5,2,4,32]{3,2,1,0:T(4,128)S(1)} %pad_maximum_fusion.50), channel_id=1, source_target_pairs={{8,0},{16,8},{24,16},{9,1},{17,9},{25,17},{10,2},{18,10},{26,18},{... | collective-permute-start | bytes 15368 | tf_op jit(solution)/shard_map/ppermute | solution.py:20
  164.7 5.8 %collective-permute-start.14 = (f32[5,6,2,32]{3,2,1,0:T(2,128)S(1)}, f32[5,6,2,32]{3,2,1,0:T(2,128)S(1)}, u32[]{:S(2)}, u32[]{:S(2)}) collective-permute-start(f32[5,6,2,32]{3,2,1,0:T(2,128)S(1)} %get-tuple-element.158), channel_id=1, source_target_pairs={{0,4},{1,5},{2,6},{3,7},{8,12},{9,13},{10,14},{11,15},{16,20},{17,... | collective-permute-start | bytes 23048 | tf_op jit(solution)/shard_map/ppermute | solution.py:19
  175.1 5.8 %collective-permute-start.17 = (f32[5,6,8,2]{3,2,1,0:T(8,128)S(1)}, f32[5,6,8,2]{3,2,1,0:T(8,128)S(1)}, u32[]{:S(2)}, u32[]{:S(2)}) collective-permute-start(f32[5,6,8,2]{3,2,1,0:T(8,128)S(1)} %get-tuple-element.151), channel_id=1, source_target_pairs={{1,0},{2,1},{3,2},{5,4},{6,5},{7,6},{9,8},{10,9},{11,10},{13,12},{... | collective-permute-start | bytes 5768 | tf_op jit(solution)/shard_map/ppermute | solution.py:20
  247.1 12.6 %collective-permute-start.18 = (f32[4,1,4,32]{3,2,1,0:T(4,128)S(1)}, f32[4,1,4,32]{3,2,1,0:T(4,128)S(1)}, u32[]{:S(2)}, u32[]{:S(2)}) collective-permute-start(f32[4,1,4,32]{3,2,1,0:T(4,128)S(1)} %get-tuple-element.175), channel_id=1, source_target_pairs={{8,0},{16,8},{24,16},{9,1},{17,9},{25,17},{10,2},{18,10},{26,18},{... | collective-permute-start | bytes 6152 | tf_op jit(solution)/shard_map/ppermute | solution.py:20
  269.5 6.2 %collective-permute-start.23 = (f32[4,4,6,1]{3,1,2,0:T(4,128)S(1)}, f32[4,4,6,1]{3,1,2,0:T(4,128)S(1)}, u32[]{:S(2)}, u32[]{:S(2)}) collective-permute-start(f32[4,4,6,1]{3,1,2,0:T(4,128)S(1)} %get-tuple-element.163), channel_id=1, source_target_pairs={{0,1},{1,2},{2,3},{4,5},{5,6},{6,7},{8,9},{9,10},{10,11},{12,13},{... | collective-permute-start | bytes 1160 | tf_op jit(solution)/shard_map/ppermute | solution.py:19
  276.6 8.8 %collective-permute-start.24 = (f32[4,1,8,64]{3,2,1,0:T(8,128)S(1)}, f32[4,1,8,64]{3,2,1,0:T(8,128)S(1)}, u32[]{:S(2)}, u32[]{:S(2)}) collective-permute-start(f32[4,1,8,64]{3,2,1,0:T(8,128)S(1)} %get-tuple-element.157), channel_id=1, source_target_pairs={{8,0},{16,8},{24,16},{9,1},{17,9},{25,17},{10,2},{18,10},{26,18},{... | collective-permute-start | bytes 24584 | tf_op jit(solution)/shard_map/ppermute | solution.py:20
  279.4 6.1 %collective-permute-start.25 = (f32[4,1,8,64]{3,2,1,0:T(8,128)S(1)}, f32[4,1,8,64]{3,2,1,0:T(8,128)S(1)}, u32[]{:S(2)}, u32[]{:S(2)}) collective-permute-start(f32[4,1,8,64]{3,2,1,0:T(8,128)S(1)} %get-tuple-element.156), channel_id=1, source_target_pairs={{0,8},{8,16},{16,24},{1,9},{9,17},{17,25},{2,10},{10,18},{18,26},{... | collective-permute-start | bytes 24584 | tf_op jit(solution)/shard_map/ppermute | solution.py:19
  292.2 5.8 %collective-permute-start.28 = (f32[4,6,10,1]{3,0,2,1:T(4,128)S(1)}, f32[4,6,10,1]{3,0,2,1:T(4,128)S(1)}, u32[]{:S(2)}, u32[]{:S(2)}) collective-permute-start(f32[4,6,10,1]{3,0,2,1:T(4,128)S(1)} %get-tuple-element.146), channel_id=1, source_target_pairs={{1,0},{2,1},{3,2},{5,4},{6,5},{7,6},{9,8},{10,9},{11,10},{13,12},{... | collective-permute-start | bytes 2888 | tf_op jit(solution)/shard_map/ppermute | solution.py:20
  295.9 6.2 %collective-permute-start.29 = (f32[4,6,10,1]{3,0,2,1:T(4,128)S(1)}, f32[4,6,10,1]{3,0,2,1:T(4,128)S(1)}, u32[]{:S(2)}, u32[]{:S(2)}) collective-permute-start(f32[4,6,10,1]{3,0,2,1:T(4,128)S(1)} %get-tuple-element.147), channel_id=1, source_target_pairs={{0,1},{1,2},{2,3},{4,5},{5,6},{6,7},{8,9},{9,10},{10,11},{12,13},{... | collective-permute-start | bytes 2888 | tf_op jit(solution)/shard_map/ppermute | solution.py:19
  307.6 10.6 %collective-permute-start.30 = (f32[4,1,16,128]{3,2,1,0:T(8,128)S(1)}, f32[4,1,16,128]{3,2,1,0:T(8,128)S(1)}, u32[]{:S(2)}, u32[]{:S(2)}) collective-permute-start(f32[4,1,16,128]{3,2,1,0:T(8,128)S(1)} %get-tuple-element.129), channel_id=1, source_target_pairs={{8,0},{16,8},{24,16},{9,1},{17,9},{25,17},{10,2},{18,10},{26,18},{... | collective-permute-start | bytes 98312 | tf_op jit(solution)/shard_map/ppermute | solution.py:20
  309.5 8.7 %collective-permute-start.31 = (f32[4,1,16,128]{3,2,1,0:T(8,128)S(1)}, f32[4,1,16,128]{3,2,1,0:T(8,128)S(1)}, u32[]{:S(2)}, u32[]{:S(2)}) collective-permute-start(f32[4,1,16,128]{3,2,1,0:T(8,128)S(1)} %get-tuple-element.128), channel_id=1, source_target_pairs={{0,8},{8,16},{16,24},{1,9},{9,17},{17,25},{2,10},{10,18},{18,26},{... | collective-permute-start | bytes 98312 | tf_op jit(solution)/shard_map/ppermute | solution.py:19
  325.3 9.9 %collective-permute-start.34 = (f32[4,10,18,1]{3,0,2,1:T(4,128)S(1)}, f32[4,10,18,1]{3,0,2,1:T(4,128)S(1)}, u32[]{:S(2)}, u32[]{:S(2)}) collective-permute-start(f32[4,10,18,1]{3,0,2,1:T(4,128)S(1)} %get-tuple-element.116), channel_id=1, source_target_pairs={{1,0},{2,1},{3,2},{5,4},{6,5},{7,6},{9,8},{10,9},{11,10},{13,12},{... | collective-permute-start | bytes 8648 | tf_op jit(solution)/shard_map/ppermute | solution.py:20
  328.9 10.3 %collective-permute-start.35 = (f32[4,10,18,1]{3,0,2,1:T(4,128)S(1)}, f32[4,10,18,1]{3,0,2,1:T(4,128)S(1)}, u32[]{:S(2)}, u32[]{:S(2)}) collective-permute-start(f32[4,10,18,1]{3,0,2,1:T(4,128)S(1)} %get-tuple-element.117), channel_id=1, source_target_pairs={{0,1},{1,2},{2,3},{4,5},{5,6},{6,7},{8,9},{9,10},{10,11},{12,13},{... | collective-permute-start | bytes 8648 | tf_op jit(solution)/shard_map/ppermute | solution.py:19
  340.0 6.4 %collective-permute-start.36 = (f32[4,1,16,128]{3,2,1,0:T(8,128)S(1)}, f32[4,1,16,128]{3,2,1,0:T(8,128)S(1)}, u32[]{:S(2)}, u32[]{:S(2)}) collective-permute-start(f32[4,1,16,128]{3,2,1,0:T(8,128)S(1)} %get-tuple-element.127), channel_id=1, source_target_pairs={{8,0},{16,8},{24,16},{9,1},{17,9},{25,17},{10,2},{18,10},{26,18},{... | collective-permute-start | bytes 98312 | tf_op jit(solution)/shard_map/ppermute | solution.py:20
  353.9 10.0 %collective-permute-start.40 = (f32[4,10,18,1]{3,0,2,1:T(4,128)S(1)}, f32[4,10,18,1]{3,0,2,1:T(4,128)S(1)}, u32[]{:S(2)}, u32[]{:S(2)}) collective-permute-start(f32[4,10,18,1]{3,0,2,1:T(4,128)S(1)} %get-tuple-element.112), channel_id=1, source_target_pairs={{1,0},{2,1},{3,2},{5,4},{6,5},{7,6},{9,8},{10,9},{11,10},{13,12},{... | collective-permute-start | bytes 8648 | tf_op jit(solution)/shard_map/ppermute | solution.py:20
  355.9 12.5 %collective-permute-start.41 = (f32[4,10,18,1]{3,0,2,1:T(4,128)S(1)}, f32[4,10,18,1]{3,0,2,1:T(4,128)S(1)}, u32[]{:S(2)}, u32[]{:S(2)}) collective-permute-start(f32[4,10,18,1]{3,0,2,1:T(4,128)S(1)} %get-tuple-element.113), channel_id=1, source_target_pairs={{0,1},{1,2},{2,3},{4,5},{5,6},{6,7},{8,9},{9,10},{10,11},{12,13},{... | collective-permute-start | bytes 8648 | tf_op jit(solution)/shard_map/ppermute | solution.py:19
  (25 other events, 175.1 us)
